TPU v7x, 128 devices: a whole 4x4x4 slice. The times are simulated.
128 devices in a mesh: seq: 16 (over x, y), tp: 8 (over z, core).
Axes of the slice: x: 4, y: 4, z: 4, core: 2. Of those that a mesh axis runs over, the one named last changes fastest.
Arguments:
- patches: bfloat16 [8192, 1280], P('seq'), may hold values from -6 to 6
- image_ids: int32 [2048], replicated, may hold values from 0 to 31, never falling along the last dimension, each value on 1 to 128 neighbouring positions
- vision_gain: float32 [1280], replicated, may hold values from 0.5 to 2
- v_query: bfloat16 [1280, 1280], P(None, 'tp'), may hold values from -0.15625 to 0.15625
- v_key: bfloat16 [1280, 1280], P(None, 'tp'), may hold values from -0.15625 to 0.15625
- v_value: bfloat16 [1280, 1280], P(None, 'tp'), may hold values from -0.15625 to 0.15625
- v_out: bfloat16 [1280, 1280], P('tp'), may hold values from -0.625 to 0.625
- merge_gain: float32 [1280], replicated, may hold values from 0.5 to 1.5
- merge_up: bfloat16 [5120, 5120], P('seq', 'tp'), may hold values from -0.078125 to 0.078125
- merge_down: bfloat16 [5120, 8192], P('tp', 'seq'), may hold values from -0.078125 to 0.078125
- owners: int32 [2048, 1], replicated, may hold values from 0 to 15; in each aligned block of 128 rows (0 to 127, 128 to 255, ...) at most 16 rows name the same one
- text_embed: bfloat16 [4096, 8192], P('seq', 'tp'), may hold values from -6 to 6
- segment_ids: int32 [4096], P('seq'), may hold values from 0 to 63, never falling along the last dimension, each value on 1 to 256 neighbouring positions
- lang_gain: float32 [8192], replicated, may hold values from 0.5 to 2
- l_query: bfloat16 [8192, 4096], P(None, 'tp'), may hold values from -0.0625 to 0.0625
- l_key: bfloat16 [8192, 1024], P(None, 'tp'), may hold values from -0.0625 to 0.0625
- l_value: bfloat16 [8192, 1024], P(None, 'tp'), may hold values from -0.0625 to 0.0625
- l_out: bfloat16 [4096, 8192], P('tp'), may hold values from -0.09375 to 0.09375
Outputs:
- layer_out: bfloat16 [4096, 8192], P('seq', 'tp')
Inputs may be any that keep to these rules, and one draw needn't show every extreme that they name: `image_ids`: never falling; each image spans 1 to 128 merged tokens, one exactly 128. `owners`: among the rows of one device (aligned blocks of 128 rows) at most 16 name the same packed sequence. `segment_ids`: never falling; each document holds 1 to 256 slots, one exactly 256.
All inputs are finite; a program needn't handle non-finite values.
Results may differ from a plain program's by a relative error of at most 0.019.
Values may be sent and summed in bfloat16 or wider, within the bound.
No kernel may reach another device: no remote copies, remote signals or barrier semaphores. Data moves between devices by JAX's collectives and lax.ppermute only.
A program may use at most 128 MiB of HBM per device.

v0:
```python
import math
import jax
import jax.numpy as jnp
from jax import lax
from jax.sharding import PartitionSpec as P

DV = 1280
VHEADS = 16
LHD = 128
EPSILON = 1e-06
NEG_FILL = -1e30


def extended(cells, sides, width):
    for axis, dim in sides:
        count = lax.axis_size(axis)
        ends = count - 1
        head = lax.slice_in_dim(cells, 0, width, axis=dim)
        tail = lax.slice_in_dim(cells, cells.shape[dim] - width, cells.shape[dim], axis=dim)
        cells = jnp.concatenate(
            [
                lax.ppermute(tail, axis, [(i, (i + 1) % count) for i in range(ends)]),
                cells,
                lax.ppermute(head, axis, [((i + 1) % count, i) for i in range(ends)]),
            ],
            axis=dim,
        )
    return cells


def split_up(value, dim, length):
    shape = value.shape
    pieces = value.reshape(*shape[:dim], length, shape[dim] // length, *shape[dim + 1 :])
    return jnp.moveaxis(pieces, dim, 0)


def sum_at_owner(value, axis, dim):
    pieces = split_up(value, dim, lax.axis_size(axis))
    arrived = lax.all_to_all(pieces, axis, split_axis=0, concat_axis=0, tiled=True)
    return arrived.astype(jnp.float32).sum(axis=0)


def from_everyone(value, axis):
    copies = jnp.broadcast_to(value, (lax.axis_size(axis), *value.shape))
    return lax.all_to_all(copies, axis, split_axis=0, concat_axis=0, tiled=True)


def of_everyone(value, axis):
    everything = from_everyone(value, axis)
    return jnp.sum(everything, axis=0)


def in_order(pieces, dim):
    pieces = jnp.moveaxis(pieces, 0, dim)
    shape = pieces.shape
    return pieces.reshape(*shape[:dim], shape[dim] * shape[dim + 1], *shape[dim + 2 :])


def gather_directly(value, axis, dim):
    pieces = from_everyone(value, axis)
    return in_order(pieces, dim)


def rms_scaled(values, norm_gain):
    mean_square = jnp.mean(values * values, axis=-1, keepdims=True)
    return (values * lax.rsqrt(mean_square + EPSILON) * norm_gain).astype(jnp.bfloat16)


def masked_attend(query_rows, key_rows, value_rows, allowed, score_scale):
    scores = (
        jnp.einsum("qhd,nhd->hqn", query_rows, key_rows, preferred_element_type=jnp.float32)
        * score_scale
    )
    scores = jnp.where(allowed[None], scores, NEG_FILL)
    highest = jnp.max(scores, axis=-1, keepdims=True)
    weights_raw = jnp.where(allowed[None], jnp.exp(scores - highest), 0.0)
    totals = jnp.sum(weights_raw, axis=-1)
    mixed = jnp.einsum(
        "hqn,nhd->qhd",
        weights_raw.astype(jnp.bfloat16),
        value_rows,
        preferred_element_type=jnp.float32,
    )
    mixed = mixed / jnp.transpose(totals)[:, :, None]
    return mixed.reshape(mixed.shape[0], -1).astype(jnp.bfloat16)


def body(
    patches,
    image_ids,
    vision_gain,
    v_query,
    v_key,
    v_value,
    v_out,
    merge_gain,
    merge_up,
    merge_down,
    owners,
    text_embed,
    segment_ids,
    lang_gain,
    l_query,
    l_key,
    l_value,
    l_out,
):
    row_count = patches.shape[0]
    local_width = v_query.shape[1]
    head_size = DV // VHEADS
    head_count = local_width // head_size
    score_scale = 1.0 / math.sqrt(head_size)
    seq_index = lax.axis_index("seq")
    patch_ids = jnp.repeat(image_ids, 4)
    my_ids = lax.dynamic_slice_in_dim(patch_ids, seq_index * row_count, row_count)
    vision_state = patches.astype(jnp.float32)
    normed = rms_scaled(vision_state, vision_gain)
    query_rows = jnp.dot(normed, v_query, preferred_element_type=jnp.float32).astype(jnp.bfloat16)
    key_part = jnp.dot(normed, v_key, preferred_element_type=jnp.float32).astype(jnp.bfloat16)
    value_part = jnp.dot(normed, v_value, preferred_element_type=jnp.float32).astype(jnp.bfloat16)
    key_value = jnp.concatenate([key_part, value_part], axis=1)
    query_grid = query_rows.reshape(row_count, head_count, head_size)
    nearby = extended(key_value, (("seq", 0),), row_count)
    padded_ids = jnp.pad(patch_ids, (row_count, row_count), constant_values=-1)
    nearby_ids = lax.dynamic_slice_in_dim(padded_ids, seq_index * row_count, 3 * row_count)
    allowed = my_ids[:, None] == nearby_ids[None, :]
    nearby_keys = nearby[:, :local_width].reshape(3 * row_count, head_count, head_size)
    nearby_values = nearby[:, local_width:].reshape(3 * row_count, head_count, head_size)
    attended = masked_attend(query_grid, nearby_keys, nearby_values, allowed, score_scale)
    partial_value = jnp.dot(attended, v_out, preferred_element_type=jnp.float32)
    share = sum_at_owner(partial_value.astype(jnp.bfloat16), "tp", 1)
    share_width = share.shape[1]
    tp_index = lax.axis_index("tp")
    own_state = (
        lax.dynamic_slice_in_dim(vision_state, tp_index * share_width, share_width, 1) + share
    )
    squares = of_everyone(jnp.sum(own_state * own_state, axis=1), "tp")
    gain_share = lax.dynamic_slice_in_dim(merge_gain, tp_index * share_width, share_width)
    normed_share = (own_state * lax.rsqrt(squares / DV + EPSILON)[:, None] * gain_share).astype(
        jnp.bfloat16
    )
    merge_normed = gather_directly(normed_share, "tp", 1)
    token_count = row_count // 4
    merge_rows = merge_normed.reshape(token_count, 4 * DV)
    hidden_sum = jnp.dot(
        merge_rows,
        lax.all_gather(merge_up, "seq", axis=0, tiled=True),
        preferred_element_type=jnp.float32,
    )
    hidden = jax.nn.gelu(hidden_sum, approximate=False).astype(jnp.bfloat16)
    down_terms = jnp.dot(
        hidden,
        lax.all_gather(merge_down, "seq", axis=1, tiled=True),
        preferred_element_type=jnp.float32,
    )
    merged = sum_at_owner(down_terms.astype(jnp.bfloat16), "tp", 1).astype(jnp.bfloat16)
    owner_count = lax.axis_size("seq")
    pair_cap = 2 * token_count // owner_count
    feature_width = merged.shape[1]
    owner_iota = jnp.arange(owner_count, dtype=jnp.int32)
    destination = owners[:, 0]
    one_hot = (destination[:, None] == owner_iota[None, :]).astype(jnp.int32)
    grid_counts = one_hot.reshape(owner_count, token_count, owner_count)
    pair_counts = jnp.sum(grid_counts, axis=1)
    mine = lax.dynamic_slice_in_dim(grid_counts, seq_index, 1, 0)[0]
    local_rank = jnp.sum((jnp.cumsum(mine, axis=0) - mine) * mine, axis=1)
    my_destination = lax.dynamic_slice_in_dim(destination, seq_index * token_count, token_count)
    send_index = my_destination * pair_cap + local_rank
    outgoing = (
        jnp.zeros((owner_count * pair_cap, feature_width), jnp.bfloat16).at[send_index].set(merged)
    )
    incoming = lax.all_to_all(
        outgoing.reshape(owner_count, pair_cap, feature_width),
        "seq",
        split_axis=0,
        concat_axis=0,
        tiled=True,
    )
    slot_count = text_embed.shape[0]
    from_each = lax.dynamic_slice_in_dim(pair_counts, seq_index, 1, 1)[:, 0]
    offsets = jnp.cumsum(from_each) - from_each
    pair_rank = jnp.arange(pair_cap, dtype=jnp.int32)
    placement = jnp.where(
        pair_rank[None, :] < from_each[:, None], offsets[:, None] + pair_rank[None, :], slot_count
    ).reshape(-1)
    vision_slots = (
        jnp.zeros((slot_count + 1, feature_width), jnp.bfloat16)
        .at[placement]
        .set(incoming.reshape(-1, feature_width))[:slot_count]
    )
    is_vision = jnp.arange(slot_count, dtype=jnp.int32) < jnp.sum(from_each)
    filled = jnp.where(is_vision[:, None], vision_slots, text_embed)
    full_rows = lax.all_gather(filled, "tp", axis=1, tiled=True)
    lang_normed = rms_scaled(full_rows.astype(jnp.float32), lang_gain)
    lang_query = jnp.dot(lang_normed, l_query, preferred_element_type=jnp.float32).astype(
        jnp.bfloat16
    )
    lang_key = jnp.dot(lang_normed, l_key, preferred_element_type=jnp.float32).astype(jnp.bfloat16)
    lang_value = jnp.dot(lang_normed, l_value, preferred_element_type=jnp.float32).astype(
        jnp.bfloat16
    )
    kv_heads = l_key.shape[1] // LHD
    group_size = l_query.shape[1] // LHD // kv_heads
    query_five = lang_query.reshape(slot_count, kv_heads, group_size, LHD)
    key_three = lang_key.reshape(slot_count, kv_heads, LHD)
    value_three = lang_value.reshape(slot_count, kv_heads, LHD)
    position = jnp.arange(slot_count, dtype=jnp.int32)
    allowed_lang = (segment_ids[:, None] == segment_ids[None, :]) & (
        position[None, :] <= position[:, None]
    )
    scores = jnp.einsum(
        "qkgd,nkd->kgqn", query_five, key_three, preferred_element_type=jnp.float32
    ) / math.sqrt(LHD)
    scores = jnp.where(allowed_lang[None, None], scores, NEG_FILL)
    highest = jnp.max(scores, axis=-1, keepdims=True)
    weights_raw = jnp.where(allowed_lang[None, None], jnp.exp(scores - highest), 0.0)
    totals = jnp.sum(weights_raw, axis=-1)
    mixed = jnp.einsum(
        "kgqn,nkd->qkgd",
        weights_raw.astype(jnp.bfloat16),
        value_three,
        preferred_element_type=jnp.float32,
    )
    mixed = mixed / jnp.transpose(totals, (2, 0, 1))[..., None]
    lang_attended = mixed.reshape(slot_count, -1).astype(jnp.bfloat16)
    out_terms = jnp.dot(lang_attended, l_out, preferred_element_type=jnp.float32)
    summed_out = lax.psum_scatter(
        out_terms.astype(jnp.bfloat16), "tp", scatter_dimension=1, tiled=True
    ).astype(jnp.float32)
    return (filled.astype(jnp.float32) + summed_out).astype(jnp.bfloat16)


def solution(mesh):
    in_specs = (
        P("seq", None),
        P(),
        P(),
        P(None, "tp"),
        P(None, "tp"),
        P(None, "tp"),
        P("tp", None),
        P(),
        P("seq", "tp"),
        P("tp", "seq"),
        P(),
        P("seq", "tp"),
        P("seq"),
        P(),
        P(None, "tp"),
        P(None, "tp"),
        P(None, "tp"),
        P("tp", None),
    )
    out_specs = P("seq", "tp")
    return jax.shard_map(body, mesh=mesh, in_specs=in_specs, out_specs=out_specs, check_vma=False)
```

profile of v0, /device:TPU:0, one launch (start us, length us, event | category | flops | bytes accessed | tf_op | source)
XLA Modules:
  0.0 336.9 jit_solution(2363182958501174080)
XLA Ops:
  13.0 4.3 %collective-permute-start = (bf16[512,320]{0,1:T(8,128)(2,1)}, bf16[512,320]{0,1:T(8,128)(2,1)}, u32[]{:S(2)}, u32[]{:S(2)}) collective-permute-start(bf16[512,320]{0,1:T(8,128)(2,1)} %pad_maximum_fusion.1), channel_id=1, source_target_pairs={{0,8},{8,16},{16,24},{24,32},{32,40},{40,48},{48,56},{56,64},{64,7... | collective-permute-start | bytes 983048 | tf_op jit(solution)/shard_map/ppermute | solution.py:22
  23.4 2.2 convolution_convert_fusion.4
  25.6 7.6 %collective-permute-done.1 = bf16[512,320]{0,1:T(8,128)(2,1)} collective-permute-done((bf16[512,320]{0,1:T(8,128)(2,1)}, bf16[512,320]{0,1:T(8,128)(2,1)}, u32[]{:S(2)}, u32[]{:S(2)}) %collective-permute-start.1) | collective-permute-done | bytes 327712 | tf_op jit(solution)/shard_map/ppermute | solution.py:24
  35.5 4.7 %fusion.135 = f32[2,512]{1,0:T(2,128)S(1)} fusion(pred[512,1536]{1,0:T(8,128)(4,1)} %broadcast_compare_fusion, bf16[512,2,80]{0,2,1:T(8,128)(2,1)} %bitcast.108, bf16[1536,2,80]{0,2,1:T(8,128)(2,1)} %bitcast.99), kind=kOutput, calls=%fused_computation.174 | convolution fusion | flops 259524096 | bytes 1445888 | tf_op jit(solution)/shard_map/sub | solution.py:76
  40.2 5.5 %fusion.19 = bf16[512,2,80]{0,2,1:T(8,128)(2,1)} fusion(bf16[1536,2,80]{0,2,1:T(8,128)(2,1)} %bitcast.101, f32[512,2]{0,1:T(2,128)S(1)} %bitcast.110, pred[512,1536]{1,0:T(8,128)(4,1)} %broadcast_compare_fusion, bf16[512,2,80]{0,2,1:T(8,128)(2,1)} %bitcast.109, bf16[1536,2,80]{0,2,1:T(8,128)(2,1)} %bitcast.100), kind=kOutput, calls=%fused_computation.32 | convolution fusion | flops 511347200 | bytes 2101248 | tf_op jit(solution)/shard_map/hqn,nhd->qhd/dot_general | solution.py:78
  45.7 2.7 convolution_convert_fusion.2
  48.4 2.4 copy.39
  50.8 6.3 %all-to-all-start = ((bf16[8,512,160]{1,2,0:T(8,128)(2,1)}), bf16[8,512,160]{1,2,0:T(8,128)(2,1)}, u32[]{:S(2)}, u32[]{:S(2)}) async-start(bf16[8,512,160]{1,2,0:T(8,128)(2,1)} %bitcast.95), calls=%async_computation | async-start | bytes 2621440 | tf_op jit(solution)/shard_map/all_to_all | solution.py:39
  59.0 17.0 %all-to-all-done = bf16[8,512,160]{1,2,0:T(8,128)(2,1)} async-done(((bf16[8,512,160]{1,2,0:T(8,128)(2,1)}), bf16[8,512,160]{1,2,0:T(8,128)(2,1)}, u32[]{:S(2)}, u32[]{:S(2)}) %all-to-all-start) | async-done | bytes 1310752 | tf_op jit(solution)/shard_map/all_to_all | solution.py:39
  79.2 3.3 all-to-all-start.1
  83.3 4.5 %all-to-all-done.1 = f32[8,1,512]{2,1,0:T(1,128)S(1)} async-done(((f32[8,1,512]{2,1,0:T(1,128)}), f32[8,1,512]{2,1,0:T(1,128)S(1)}, u32[]{:S(2)}, u32[]{:S(2)}) %all-to-all-start.1) | async-done | bytes 16416 | tf_op jit(solution)/shard_map/all_to_all | solution.py:45
  89.0 21.2 %all_to_all.26 = bf16[8,512,160]{1,2,0:T(8,128)(2,1)S(1)} all-to-all(bf16[8,512,160]{1,2,0:T(8,128)(2,1)S(1)} %broadcast_in_dim.99), channel_id=1, replica_groups=mesh['seq'=16,'tp'=8] {'tp'}, dimensions={0} | all-to-all | bytes 2621440 | tf_op jit(solution)/shard_map/all_to_all | solution.py:45
  110.2 3.0 copy.41
  113.2 4.4 %reshape_reshape.3 = bf16[128,5120]{1,0:T(8,128)(2,1)S(1)} reshape(bf16[512,8,160]{2,1,0:T(8,128)(2,1)} %copy.41) | data formatting | bytes 2621440 | tf_op jit(solution)/shard_map/reshape;reshape | solution.py:144
  117.7 48.6 %all-gather.6.cloned.1.call-done = bf16[640,8192]{1,0:T(8,128)(2,1)} async-done(((bf16[640,512]{1,0:T(8,128)(2,1)}), bf16[640,8192]{1,0:T(8,128)(2,1)}) %all-gather.6.cloned.1.call-update) | async-done | bytes 10485776 | tf_op jit(solution)/shard_map/all_gather | solution.py:153
  166.3 10.7 %convolution_convert_fusion.1 = bf16[128,8192]{1,0:T(8,128)(2,1)} fusion(bf16[640,8192]{1,0:T(8,128)(2,1)} %all-gather.6.cloned.1.call-done, bf16[128,5120]{1,0:T(8,128)(2,1)S(1)} %reshape_reshape.3, bf16[5120,640]{1,0:T(8,128)(2,1)} %all-gather.4.cloned.1.call-done), kind=kOutput, calls=%fused_computation.6 | convolution fusion | flops 2187411456 | bytes 20447232 | tf_op jit(solution)/shard_map/dot_general | solution.py:151
  177.1 3.2 copy.59
  180.3 4.6 %all-to-all-start.3 = ((bf16[8,128,1024]{2,1,0:T(8,128)(2,1)}), bf16[8,128,1024]{2,1,0:T(8,128)(2,1)}, u32[]{:S(2)}, u32[]{:S(2)}) async-start(bf16[8,128,1024]{2,1,0:T(8,128)(2,1)} %bitcast.94), calls=%async_computation.3 | async-start | bytes 4194304 | tf_op jit(solution)/shard_map/all_to_all | solution.py:39
  186.7 25.4 %all-to-all-done.3 = bf16[8,128,1024]{2,1,0:T(8,128)(2,1)} async-done(((bf16[8,128,1024]{2,1,0:T(8,128)(2,1)}), bf16[8,128,1024]{2,1,0:T(8,128)(2,1)}, u32[]{:S(2)}, u32[]{:S(2)}) %all-to-all-start.3) | async-done | bytes 2097184 | tf_op jit(solution)/shard_map/all_to_all | solution.py:39
  212.1 2.0 reduce_sum.115
  214.1 2.0 scatter_custom_fusion
  216.0 4.9 %all-to-all-start.4 = ((bf16[16,16,1024]{2,1,0:T(8,128)(2,1)}), bf16[16,16,1024]{2,1,0:T(8,128)(2,1)S(1)}, u32[]{:S(2)}, u32[]{:S(2)}) async-start(bf16[16,16,1024]{2,1,0:T(8,128)(2,1)} %bitcast.15), calls=%async_computation.4 | async-start | bytes 1048576 | tf_op jit(solution)/shard_map/all_to_all | solution.py:172
  221.8 10.3 %all-to-all-done.4 = bf16[16,16,1024]{2,1,0:T(8,128)(2,1)S(1)} async-done(((bf16[16,16,1024]{2,1,0:T(8,128)(2,1)}), bf16[16,16,1024]{2,1,0:T(8,128)(2,1)S(1)}, u32[]{:S(2)}, u32[]{:S(2)}) %all-to-all-start.4) | async-done | bytes 524320 | tf_op jit(solution)/shard_map/all_to_all | solution.py:172
  232.9 2.3 scatter_custom_fusion.1
  236.6 28.0 %all-gather.8.cloned.1.call-done = bf16[256,8192]{1,0:T(8,128)(2,1)} async-done(((bf16[256,1024]{1,0:T(8,128)(2,1)}), bf16[256,8192]{1,0:T(8,128)(2,1)}) %all-gather.8.cloned.1.call-update) | async-done | bytes 4194320 | tf_op jit(solution)/shard_map/all_gather | solution.py:193
  264.6 3.3 fusion.1
  268.1 5.8 %fusion.18 = bf16[32,4,8,128]{3,2,1,0:T(8,128)(2,1)S(1)} fusion(bf16[8192,512]{1,0:T(8,128)(2,1)} %param.32, bf16[256,8192]{1,0:T(8,128)(2,1)S(1)} %copy-done.2, f32[8192]{0:T(1024)S(1)} %copy-done.13, f32[256]{0:T(256)S(1)} %add_rsqrt_fusion.2), kind=kOutput, calls=%fused_computation.31 | convolution fusion | flops 2156003328 | bytes 12878848 | tf_op jit(solution)/shard_map/dot_general | solution.py:195
  273.9 3.8 %fusion.136 = (f32[4,256]{1,0:T(4,128)S(1)}, f32[1,4,256,256]{2,3,1,0:T(8,128)S(1)}) fusion(bf16[32,4,8,128]{3,2,1,0:T(8,128)(2,1)S(1)} %fusion.18, bf16[8192,128]{1,0:T(8,128)(2,1)S(1)} %copy-done, bf16[256,8192]{1,0:T(8,128)(2,1)} %all-gather.8.cloned.1.call-done, f32[8192]{0:T(1024)S(1)} %copy-done.13, f32[256]{0:T(256)S(1)} %add_rsqrt_fusion.2, ...), kind=kOutput, calls=%fused_computation.175 | convolution fusion | flops 613186560 | bytes 7705600 | tf_op jit(solution)/shard_map/qkgd,nkd->kgqn/dot_general | solution.py:211
  277.9 4.5 %fusion.28 = bf16[256,1,4,128]{0,3,2,1:T(8,128)(2,1)S(1)} fusion(bf16[8192,128]{1,0:T(8,128)(2,1)} %param.34, f32[1,4,256,256]{2,3,1,0:T(8,128)S(1)} %get-tuple-element.11, f32[4,256]{1,0:T(4,128)S(1)} %get-tuple-element.10, pred[256,256]{0,1:T(8,128)(4,1)S(1)} %fusion.53, f32[256,4]{0,1:T(4,128)S(1)} %bitcast.106, ...), kind=kOutput, calls=%fused_computation.46 | convolution fusion | flops 613449728 | bytes 7709696 | tf_op jit(solution)/shard_map/kgqn,nkd->qkgd/dot_general | solution.py:218
  282.5 7.7 %convolution_convert_fusion = bf16[256,8192]{1,0:T(8,128)(2,1)} fusion(bf16[256,512]{0,1:T(8,128)(2,1)S(1)} %bitcast.102, bf16[512,8192]{1,0:T(8,128)(2,1)} %param.35), kind=kOutput, calls=%fused_computation.5 | convolution fusion | flops 2149580800 | bytes 12845056 | tf_op jit(solution)/shard_map/dot_general | solution.py:226
  290.2 38.1 %reduce-scatter.2.cloned.1.call-done = bf16[256,1024]{1,0:T(8,128)(2,1)} async-done(((bf16[256,8192]{1,0:T(8,128)(2,1)}), bf16[256,1024]{1,0:T(8,128)(2,1)}) %reduce-scatter.2.cloned.1.call-update) | async-done | bytes 524304 | tf_op jit(solution)/shard_map/reduce_scatter | solution.py:227
  328.3 2.0 add_convert_fusion
  (80 shorter events, 27.0 us)
Async XLA Ops:
  6.5 267.3 %copy-start = (bf16[8192,128]{1,0:T(8,128)(2,1)S(1)}, bf16[8192,128]{1,0:T(8,128)(2,1)}, u32[]{:S(2)}) copy-start(bf16[8192,128]{1,0:T(8,128)(2,1)} %param.33) | copy-start | bytes 6291460
  6.5 3.5 %copy-start.14 = (f32[1280]{0:T(1024)S(1)}, f32[1280]{0:T(1024)}, u32[]{:S(2)}) copy-start(f32[1280]{0:T(1024)} %param.20) | copy-start | bytes 15364
  6.5 111.1 %all-gather.4.cloned.1.call-start = ((), (), s32[]{:S(2)}) async-start(), calls=%async_computation.6 | async-start | bytes 6963200 | tf_op jit(solution)/shard_map/all_gather | solution.py:147
  7.3 159.1 %all-gather.6.cloned.1.call-start = ((), (), s32[]{:S(2)}) async-start(), calls=%async_computation.7 | async-start | bytes 11141120 | tf_op jit(solution)/shard_map/all_gather | solution.py:153
  9.6 1.9 copy-start.12
  10.0 8.6 %copy-start.10 = (s32[2048]{0:T(1024)S(1)}, s32[2048]{0:T(1024)}, u32[]{:S(2)}) copy-start(s32[2048]{0:T(1024)} %param.19) | copy-start | bytes 24580
  11.6 0.7 copy-start.3
  12.2 0.8 copy-start.5
  13.0 12.6 %collective-permute-start = (bf16[512,320]{0,1:T(8,128)(2,1)}, bf16[512,320]{0,1:T(8,128)(2,1)}, u32[]{:S(2)}, u32[]{:S(2)}) collective-permute-start(bf16[512,320]{0,1:T(8,128)(2,1)} %pad_maximum_fusion.1), channel_id=1, source_target_pairs={{0,8},{8,16},{16,24},{24,32},{32,40},{40,48},{48,56},{56,64},{64,7... | collective-permute-start | bytes 983048 | tf_op jit(solution)/shard_map/ppermute | solution.py:22
  17.3 16.0 %collective-permute-start.1 = (bf16[512,320]{0,1:T(8,128)(2,1)}, bf16[512,320]{0,1:T(8,128)(2,1)}, u32[]{:S(2)}, u32[]{:S(2)}) collective-permute-start(bf16[512,320]{0,1:T(8,128)(2,1)} %pad_maximum_fusion.1), channel_id=1, source_target_pairs={{8,0},{16,8},{24,16},{32,24},{40,32},{48,40},{56,48},{64,56},{72,6... | collective-permute-start | bytes 983048 | tf_op jit(solution)/shard_map/ppermute | solution.py:24
  21.8 11.5 %copy-start.4 = (bf16[512,160]{0,1:T(8,128)(2,1)S(1)}, bf16[512,160]{0,1:T(8,128)(2,1)}, u32[]{:S(2)}) copy-start(bf16[512,160]{0,1:T(8,128)(2,1)} %copy-done.3) | copy-start | bytes 491524
  21.8 11.5 %copy-start.6 = (bf16[512,160]{0,1:T(8,128)(2,1)S(1)}, bf16[512,160]{0,1:T(8,128)(2,1)}, u32[]{:S(2)}) copy-start(bf16[512,160]{0,1:T(8,128)(2,1)} %copy-done.5) | copy-start | bytes 491524
  50.8 25.1 %all-to-all-start = ((bf16[8,512,160]{1,2,0:T(8,128)(2,1)}), bf16[8,512,160]{1,2,0:T(8,128)(2,1)}, u32[]{:S(2)}, u32[]{:S(2)}) async-start(bf16[8,512,160]{1,2,0:T(8,128)(2,1)} %bitcast.95), calls=%async_computation | async-start | bytes 2621440 | tf_op jit(solution)/shard_map/all_to_all | solution.py:39
  79.2 8.6 %all-to-all-start.1 = ((f32[8,1,512]{2,1,0:T(1,128)}), f32[8,1,512]{2,1,0:T(1,128)S(1)}, u32[]{:S(2)}, u32[]{:S(2)}) async-start(f32[8,1,512]{2,1,0:T(1,128)} %broadcast_in_dim.98), calls=%async_computation.1 | async-start | bytes 32768 | tf_op jit(solution)/shard_map/all_to_all | solution.py:45
  180.3 4.6 %copy-start.9 = (s32[2048,1]{0,1:T(1,128)S(1)}, s32[2048,1]{0,1:T(1,128)}, u32[]{:S(2)}) copy-start(s32[2048,1]{0,1:T(1,128)} %param.28) | copy-start | bytes 24580
  180.3 31.8 %all-to-all-start.3 = ((bf16[8,128,1024]{2,1,0:T(8,128)(2,1)}), bf16[8,128,1024]{2,1,0:T(8,128)(2,1)}, u32[]{:S(2)}, u32[]{:S(2)}) async-start(bf16[8,128,1024]{2,1,0:T(8,128)(2,1)} %bitcast.94), calls=%async_computation.3 | async-start | bytes 4194304 | tf_op jit(solution)/shard_map/all_to_all | solution.py:39
  186.7 48.6 %copy-start.7 = (bf16[256,1024]{1,0:T(8,128)(2,1)S(1)}, bf16[256,1024]{1,0:T(8,128)(2,1)}, u32[]{:S(2)}) copy-start(bf16[256,1024]{1,0:T(8,128)(2,1)} %param.29) | copy-start | bytes 1572868
  186.7 49.8 %copy-start.11 = (s32[256]{0:T(256)S(1)}, s32[256]{0:T(256)}, u32[]{:S(2)}) copy-start(s32[256]{0:T(256)} %param.30) | copy-start | bytes 3076
  216.0 16.1 %all-to-all-start.4 = ((bf16[16,16,1024]{2,1,0:T(8,128)(2,1)}), bf16[16,16,1024]{2,1,0:T(8,128)(2,1)S(1)}, u32[]{:S(2)}, u32[]{:S(2)}) async-start(bf16[16,16,1024]{2,1,0:T(8,128)(2,1)} %bitcast.15), calls=%async_computation.4 | async-start | bytes 1048576 | tf_op jit(solution)/shard_map/all_to_all | solution.py:172
  221.0 43.6 %all-gather.8.cloned.1.call-start = ((), (), s32[]{:S(2)}) async-start(), calls=%async_computation.8 | async-start | bytes 4718592 | tf_op jit(solution)/shard_map/all_gather | solution.py:193
  232.2 0.8 copy-start.8
  235.3 32.6 %copy-start.13 = (f32[8192]{0:T(1024)S(1)}, f32[8192]{0:T(1024)}, u32[]{:S(2)}) copy-start(f32[8192]{0:T(1024)} %param.31) | copy-start | bytes 98308
  236.2 92.1 %reduce-scatter.2.cloned.1.call-start = ((), (), s32[]{:S(2)}) async-start(), calls=%async_computation.9 | async-start | bytes 4718592 | tf_op jit(solution)/shard_map/reduce_scatter | solution.py:227
  264.6 3.4 %copy-start.2 = (bf16[256,8192]{1,0:T(8,128)(2,1)S(1)}, bf16[256,8192]{1,0:T(8,128)(2,1)}, u32[]{:S(2)}) copy-start(bf16[256,8192]{1,0:T(8,128)(2,1)} %all-gather.8.cloned.1.call-done) | copy-start | bytes 12582916
  290.2 38.2 %copy-start.1 = (bf16[256,1024]{1,0:T(8,128)(2,1)S(1)}, bf16[256,1024]{1,0:T(8,128)(2,1)}, u32[]{:S(2)}) copy-start(bf16[256,1024]{1,0:T(8,128)(2,1)} %slice_select_fusion) | copy-start | bytes 1572868
Sparse Core Ops, SparseCore 0:
  9.5 67.2 all-gather.3
  78.9 87.3 all-gather.5
  236.3 28.2 all-gather.7
  290.3 37.9 reduce-scatter.1
where the time goes:
time: 338 us; the launch traced here: 337 us
  waiting for transfers between devices  181 us (54%)
  matrix products  49.8 us (15%)
  local copies, waits for them, and re-layouts  26.1 us (8%)
  starting transfers between devices  25.1 us (7%)
  blocking collectives  21.2 us (6%)
  other arithmetic  20.2 us (6%)
  between operations  13.4 us (4%)
    all_gather x1, waiting for transfers between devices, body(): lax.all_gather(merge_down, 'seq', axis=1, tiled=True)  48.6 us
    all_to_all x2, waiting for transfers between devices, sum_at_owner(): lax.all_to_all(pieces, axis, split_axis=0, concat_axis=0, tiled=True)  42.3 us
    reduce_scatter x1, waiting for transfers between devices, body(): lax.psum_scatter(out_terms.astype(jnp.bfloat16), 'tp', scatter_dimension=...  38.1 us
    all_gather x1, waiting for transfers between devices, body(): full_rows = lax.all_gather(filled, 'tp', axis=1, tiled=True)  28 us
    all_to_all x1, blocking collectives, from_everyone(): return lax.all_to_all(copies, axis, split_axis=0, concat_axis=0, tiled=True)  21.2 us
    all_to_all x2, starting transfers between devices, sum_at_owner(): lax.all_to_all(pieces, axis, split_axis=0, concat_axis=0, tiled=True)  10.8 us
    dot_general x1, matrix products, body(): jnp.dot(hidden, lax.all_gather(merge_down, 'seq', axis=1, tiled=True), pr...  10.7 us
    all_to_all x1, waiting for transfers between devices, body(): lax.all_to_all(outgoing.reshape(owner_count, pair_cap, feature_width), 's...  10.3 us
  transfers between devices with their start and end apart: 10, of which 9 were waited for; matrix products, arithmetic and copies ran while one was open for 14% of the time, Pallas kernels for 0%

commit v1 on v0

--- a/solution.py
+++ b/solution.py
@@ -9,6 +9,15 @@
 LHD = 128
 EPSILON = 1e-06
 NEG_FILL = -1e30
+_extend_chunk = lambda matrix, bus_axis: jnp.concatenate(
+    lax.all_to_all(
+        jnp.stack([matrix] * lax.axis_size(bus_axis)),
+        concat_axis=0,
+        axis_name=bus_axis,
+        split_axis=0,
+    ),
+    axis=1,
+)
 
 
 def extended(cells, sides, width):
@@ -190,7 +199,7 @@
     )
     is_vision = jnp.arange(slot_count, dtype=jnp.int32) < jnp.sum(from_each)
     filled = jnp.where(is_vision[:, None], vision_slots, text_embed)
-    full_rows = lax.all_gather(filled, "tp", axis=1, tiled=True)
+    full_rows = _extend_chunk(filled, "tp")
     lang_normed = rms_scaled(full_rows.astype(jnp.float32), lang_gain)
     lang_query = jnp.dot(lang_normed, l_query, preferred_element_type=jnp.float32).astype(
         jnp.bfloat16

time: 338 us -> 368 us (1.089)
  waiting for transfers between devices: 181 us -> 199 us
  starting transfers between devices: 25.1 us -> 29.7 us
  other arithmetic: 20.2 us -> 24.6 us
    all_to_all x0 -> x1, waiting for transfers between devices: none -> 49.2 us  [lax.all_to_all(jnp.stack([matrix] * lax.axis_size(bus_axis)), concat_axis...]
    all_gather x1 -> x0, waiting for transfers between devices: 28 us -> none  [body(): full_rows = lax.all_gather(filled, 'tp', axis=1, tiled=True)]
    all_to_all x0 -> x1, starting transfers between devices: none -> 4.68 us  [lax.all_to_all(jnp.stack([matrix] * lax.axis_size(bus_axis)), concat_axis...]
    reduce_scatter x1, waiting for transfers between devices: 38.1 us -> 34.3 us  [body(): lax.psum_scatter(out_terms.astype(jnp.bfloat16), 'tp', scatter_dimension=...]
  transfers between devices with their start and end apart: 10 -> 10, of which waited for: 9 -> 9; matrix products, arithmetic and copies ran while one was open for 14% -> 13% of each run, Pallas kernels for 0% -> 0%
where the time goes in v1:
time: 368 us; the launch traced here: 367 us
  waiting for transfers between devices  199 us (54%)
  matrix products  50.6 us (14%)
  starting transfers between devices  29.7 us (8%)
  local copies, waits for them, and re-layouts  28.9 us (8%)
  other arithmetic  24.6 us (7%)
  blocking collectives  21.2 us (6%)
  between operations  13.4 us (4%)
    all_to_all x1, waiting for transfers between devices, lax.all_to_all(jnp.stack([matrix] * lax.axis_size(bus_axis)), concat_axis...  49.2 us
    all_gather x1, waiting for transfers between devices, body(): lax.all_gather(merge_down, 'seq', axis=1, tiled=True)  48.6 us
    all_to_all x2, waiting for transfers between devices, sum_at_owner(): lax.all_to_all(pieces, axis, split_axis=0, concat_axis=0, tiled=True)  42.4 us
    reduce_scatter x1, waiting for transfers between devices, body(): lax.psum_scatter(out_terms.astype(jnp.bfloat16), 'tp', scatter_dimension=...  34.3 us
    all_to_all x1, blocking collectives, from_everyone(): return lax.all_to_all(copies, axis, split_axis=0, concat_axis=0, tiled=True)  21.2 us
    all_to_all x2, starting transfers between devices, sum_at_owner(): lax.all_to_all(pieces, axis, split_axis=0, concat_axis=0, tiled=True)  10.8 us
    dot_general x1, matrix products, body(): jnp.dot(hidden, lax.all_gather(merge_down, 'seq', axis=1, tiled=True), pr...  10.7 us
    all_to_all x1, waiting for transfers between devices, body(): lax.all_to_all(outgoing.reshape(owner_count, pair_cap, feature_width), 's...  10.4 us
  transfers between devices with their start and end apart: 10, of which 9 were waited for; matrix products, arithmetic and copies ran while one was open for 13% of the time, Pallas kernels for 0%

profile of v1, /device:TPU:0, one launch (start us, length us, event | category | flops | bytes accessed | tf_op | source)
XLA Modules:
  0.0 367.1 jit_solution(5451829484039944341)
XLA Ops:
  13.0 4.3 %collective-permute-start = (bf16[512,320]{0,1:T(8,128)(2,1)}, bf16[512,320]{0,1:T(8,128)(2,1)}, u32[]{:S(2)}, u32[]{:S(2)}) collective-permute-start(bf16[512,320]{0,1:T(8,128)(2,1)} %pad_maximum_fusion.1), channel_id=1, source_target_pairs={{0,8},{8,16},{16,24},{24,32},{32,40},{40,48},{48,56},{56,64},{64,7... | collective-permute-start | bytes 983048 | tf_op jit(solution)/shard_map/ppermute | solution.py:31
  23.4 2.2 convolution_convert_fusion.4
  25.6 7.6 %collective-permute-done.1 = bf16[512,320]{0,1:T(8,128)(2,1)} collective-permute-done((bf16[512,320]{0,1:T(8,128)(2,1)}, bf16[512,320]{0,1:T(8,128)(2,1)}, u32[]{:S(2)}, u32[]{:S(2)}) %collective-permute-start.1) | collective-permute-done | bytes 327712 | tf_op jit(solution)/shard_map/ppermute | solution.py:33
  35.5 4.7 %fusion.129 = f32[2,512]{1,0:T(2,128)S(1)} fusion(pred[512,1536]{1,0:T(8,128)(4,1)} %broadcast_compare_fusion, bf16[512,2,80]{0,2,1:T(8,128)(2,1)} %bitcast.119, bf16[1536,2,80]{0,2,1:T(8,128)(2,1)} %bitcast.110), kind=kOutput, calls=%fused_computation.173 | convolution fusion | flops 259524096 | bytes 1445888 | tf_op jit(solution)/shard_map/sub | solution.py:85
  40.2 5.5 %fusion.18 = bf16[512,2,80]{0,2,1:T(8,128)(2,1)} fusion(bf16[1536,2,80]{0,2,1:T(8,128)(2,1)} %bitcast.112, f32[512,2]{0,1:T(2,128)S(1)} %bitcast.121, pred[512,1536]{1,0:T(8,128)(4,1)} %broadcast_compare_fusion, bf16[512,2,80]{0,2,1:T(8,128)(2,1)} %bitcast.120, bf16[1536,2,80]{0,2,1:T(8,128)(2,1)} %bitcast.111), kind=kOutput, calls=%fused_computation.31 | convolution fusion | flops 511347200 | bytes 2101248 | tf_op jit(solution)/shard_map/hqn,nhd->qhd/dot_general | solution.py:87
  45.7 2.7 convolution_convert_fusion.2
  48.4 2.4 copy.42
  50.8 6.3 %all-to-all-start = ((bf16[8,512,160]{1,2,0:T(8,128)(2,1)}), bf16[8,512,160]{1,2,0:T(8,128)(2,1)}, u32[]{:S(2)}, u32[]{:S(2)}) async-start(bf16[8,512,160]{1,2,0:T(8,128)(2,1)} %bitcast.106), calls=%async_computation | async-start | bytes 2621440 | tf_op jit(solution)/shard_map/all_to_all | solution.py:48
  59.0 17.0 %all-to-all-done = bf16[8,512,160]{1,2,0:T(8,128)(2,1)} async-done(((bf16[8,512,160]{1,2,0:T(8,128)(2,1)}), bf16[8,512,160]{1,2,0:T(8,128)(2,1)}, u32[]{:S(2)}, u32[]{:S(2)}) %all-to-all-start) | async-done | bytes 1310752 | tf_op jit(solution)/shard_map/all_to_all | solution.py:48
  79.2 3.3 all-to-all-start.1
  83.3 4.5 %all-to-all-done.1 = f32[8,1,512]{2,1,0:T(1,128)S(1)} async-done(((f32[8,1,512]{2,1,0:T(1,128)}), f32[8,1,512]{2,1,0:T(1,128)S(1)}, u32[]{:S(2)}, u32[]{:S(2)}) %all-to-all-start.1) | async-done | bytes 16416 | tf_op jit(solution)/shard_map/all_to_all | solution.py:54
  89.0 21.2 %all_to_all.31 = bf16[8,512,160]{1,2,0:T(8,128)(2,1)S(1)} all-to-all(bf16[8,512,160]{1,2,0:T(8,128)(2,1)S(1)} %broadcast_in_dim.99), channel_id=1, replica_groups=mesh['seq'=16,'tp'=8] {'tp'}, dimensions={0} | all-to-all | bytes 2621440 | tf_op jit(solution)/shard_map/all_to_all | solution.py:54
  110.2 3.0 copy.44
  113.2 4.4 %reshape_reshape.3 = bf16[128,5120]{1,0:T(8,128)(2,1)S(1)} reshape(bf16[512,8,160]{2,1,0:T(8,128)(2,1)} %copy.44) | data formatting | bytes 2621440 | tf_op jit(solution)/shard_map/reshape;reshape | solution.py:153
  117.7 48.6 %all-gather.5.cloned.1.call-done = bf16[640,8192]{1,0:T(8,128)(2,1)} async-done(((bf16[640,512]{1,0:T(8,128)(2,1)}), bf16[640,8192]{1,0:T(8,128)(2,1)}) %all-gather.5.cloned.1.call-update) | async-done | bytes 10485776 | tf_op jit(solution)/shard_map/all_gather | solution.py:162
  166.3 10.7 %convolution_convert_fusion.1 = bf16[128,8192]{1,0:T(8,128)(2,1)} fusion(bf16[640,8192]{1,0:T(8,128)(2,1)} %all-gather.5.cloned.1.call-done, bf16[128,5120]{1,0:T(8,128)(2,1)S(1)} %reshape_reshape.3, bf16[5120,640]{1,0:T(8,128)(2,1)} %all-gather.3.cloned.1.call-done), kind=kOutput, calls=%fused_computation.4 | convolution fusion | flops 2187411456 | bytes 20447232 | tf_op jit(solution)/shard_map/dot_general | solution.py:160
  177.1 3.2 copy.63
  180.3 4.6 %all-to-all-start.3 = ((bf16[8,128,1024]{2,1,0:T(8,128)(2,1)}), bf16[8,128,1024]{2,1,0:T(8,128)(2,1)}, u32[]{:S(2)}, u32[]{:S(2)}) async-start(bf16[8,128,1024]{2,1,0:T(8,128)(2,1)} %bitcast.105), calls=%async_computation.3 | async-start | bytes 4194304 | tf_op jit(solution)/shard_map/all_to_all | solution.py:48
  186.7 25.4 %all-to-all-done.3 = bf16[8,128,1024]{2,1,0:T(8,128)(2,1)} async-done(((bf16[8,128,1024]{2,1,0:T(8,128)(2,1)}), bf16[8,128,1024]{2,1,0:T(8,128)(2,1)}, u32[]{:S(2)}, u32[]{:S(2)}) %all-to-all-start.3) | async-done | bytes 2097184 | tf_op jit(solution)/shard_map/all_to_all | solution.py:48
  216.0 4.9 %all-to-all-start.4 = ((bf16[16,16,1024]{2,1,0:T(8,128)(2,1)}), bf16[16,16,1024]{2,1,0:T(8,128)(2,1)S(1)}, u32[]{:S(2)}, u32[]{:S(2)}) async-start(bf16[16,16,1024]{2,1,0:T(8,128)(2,1)} %bitcast.15), calls=%async_computation.4 | async-start | bytes 1048576 | tf_op jit(solution)/shard_map/all_to_all | solution.py:181
  221.8 10.4 %all-to-all-done.4 = bf16[16,16,1024]{2,1,0:T(8,128)(2,1)S(1)} async-done(((bf16[16,16,1024]{2,1,0:T(8,128)(2,1)}), bf16[16,16,1024]{2,1,0:T(8,128)(2,1)S(1)}, u32[]{:S(2)}, u32[]{:S(2)}) %all-to-all-start.4) | async-done | bytes 524320 | tf_op jit(solution)/shard_map/all_to_all | solution.py:181
  235.3 2.2 stack.2
  237.6 4.7 %all-to-all-start.5 = ((bf16[8,256,1024]{1,2,0:T(8,128)(2,1)}), bf16[8,256,1024]{1,2,0:T(8,128)(2,1)}, u32[]{:S(2)}, u32[]{:S(2)}) async-start(bf16[8,256,1024]{1,2,0:T(8,128)(2,1)} %stack.2), calls=%async_computation.5 | async-start | bytes 8388608 | tf_op jit(solution)/shard_map/all_to_all | solution.py:13
  242.7 49.2 %all-to-all-done.5 = bf16[8,256,1024]{1,2,0:T(8,128)(2,1)} async-done(((bf16[8,256,1024]{1,2,0:T(8,128)(2,1)}), bf16[8,256,1024]{1,2,0:T(8,128)(2,1)}, u32[]{:S(2)}, u32[]{:S(2)}) %all-to-all-start.5) | async-done | bytes 4194336 | tf_op jit(solution)/shard_map/all_to_all | solution.py:13
  291.9 3.3 multiply_reduce_fusion
  295.2 2.9 fusion.2
  300.0 5.7 %fusion.17 = bf16[32,4,8,128]{3,2,1,0:T(8,128)(2,1)S(1)} fusion(bf16[256,8192]{0,1:T(8,128)(2,1)S(1)} %fusion.2, bf16[8192,512]{1,0:T(8,128)(2,1)} %param.32), kind=kOutput, calls=%fused_computation.30 | convolution fusion | flops 2147614720 | bytes 12845056 | tf_op jit(solution)/shard_map/dot_general | solution.py:204
  305.7 4.7 %fusion.130 = (f32[4,256]{1,0:T(4,128)S(1)}, f32[1,4,256,256]{2,3,1,0:T(8,128)}) fusion(bf16[32,4,8,128]{3,2,1,0:T(8,128)(2,1)S(1)} %fusion.17, bf16[256,8192]{0,1:T(8,128)(2,1)} %copy-done.1, bf16[8192,128]{1,0:T(8,128)(2,1)S(1)} %copy-done, pred[256,256]{0,1:T(8,128)(4,1)S(1)} %fusion.52), kind=kOutput, calls=%fused_computation.174 | convolution fusion | flops 604797952 | bytes 7671808 | tf_op jit(solution)/shard_map/qkgd,nkd->kgqn/dot_general | solution.py:220
  311.9 4.6 %fusion.27 = bf16[256,1,4,128]{0,3,2,1:T(8,128)(2,1)S(1)} fusion(bf16[256,8192]{0,1:T(8,128)(2,1)} %copy-done.1, bf16[8192,128]{1,0:T(8,128)(2,1)} %param.34, f32[1,4,256,256]{2,3,1,0:T(8,128)} %get-tuple-element.11, f32[4,256]{1,0:T(4,128)S(1)} %get-tuple-element.10, pred[256,256]{0,1:T(8,128)(4,1)S(1)} %fusion.52, f32[256,4]{0,1:T(4,128)S(1)} %bitcast.117), kind=kOutput, calls=%fused_computation.45 | convolution fusion | flops 605061120 | bytes 7675904 | tf_op jit(solution)/shard_map/kgqn,nkd->qkgd/dot_general | solution.py:227
  316.5 7.7 %convolution_convert_fusion = bf16[256,8192]{1,0:T(8,128)(2,1)} fusion(bf16[256,512]{0,1:T(8,128)(2,1)S(1)} %bitcast.113, bf16[512,8192]{1,0:T(8,128)(2,1)} %param.35), kind=kOutput, calls=%fused_computation.3 | convolution fusion | flops 2149580800 | bytes 12845056 | tf_op jit(solution)/shard_map/dot_general | solution.py:235
  324.2 34.3 %reduce-scatter.2.cloned.1.call-done = bf16[256,1024]{1,0:T(8,128)(2,1)} async-done(((bf16[256,8192]{1,0:T(8,128)(2,1)}), bf16[256,1024]{1,0:T(8,128)(2,1)}) %reduce-scatter.2.cloned.1.call-update) | async-done | bytes 524304 | tf_op jit(solution)/shard_map/reduce_scatter | solution.py:236
  358.5 2.0 add_convert_fusion
  (76 shorter events, 35.2 us)
Async XLA Ops:
  6.5 299.2 %copy-start = (bf16[8192,128]{1,0:T(8,128)(2,1)S(1)}, bf16[8192,128]{1,0:T(8,128)(2,1)}, u32[]{:S(2)}) copy-start(bf16[8192,128]{1,0:T(8,128)(2,1)} %param.33) | copy-start | bytes 6291460
  6.5 3.5 copy-start.11
  6.5 111.1 %all-gather.3.cloned.1.call-start = ((), (), s32[]{:S(2)}) async-start(), calls=%async_computation.7 | async-start | bytes 6963200 | tf_op jit(solution)/shard_map/all_gather | solution.py:156
  7.3 159.1 %all-gather.5.cloned.1.call-start = ((), (), s32[]{:S(2)}) async-start(), calls=%async_computation.8 | async-start | bytes 11141120 | tf_op jit(solution)/shard_map/all_gather | solution.py:162
  9.6 1.9 copy-start.10
  10.0 8.6 %copy-start.8 = (s32[2048]{0:T(1024)S(1)}, s32[2048]{0:T(1024)}, u32[]{:S(2)}) copy-start(s32[2048]{0:T(1024)} %param.19) | copy-start | bytes 24580
  11.6 0.7 copy-start.2
  12.2 0.8 copy-start.4
  13.0 12.6 %collective-permute-start = (bf16[512,320]{0,1:T(8,128)(2,1)}, bf16[512,320]{0,1:T(8,128)(2,1)}, u32[]{:S(2)}, u32[]{:S(2)}) collective-permute-start(bf16[512,320]{0,1:T(8,128)(2,1)} %pad_maximum_fusion.1), channel_id=1, source_target_pairs={{0,8},{8,16},{16,24},{24,32},{32,40},{40,48},{48,56},{56,64},{64,7... | collective-permute-start | bytes 983048 | tf_op jit(solution)/shard_map/ppermute | solution.py:31
  17.3 16.0 %collective-permute-start.1 = (bf16[512,320]{0,1:T(8,128)(2,1)}, bf16[512,320]{0,1:T(8,128)(2,1)}, u32[]{:S(2)}, u32[]{:S(2)}) collective-permute-start(bf16[512,320]{0,1:T(8,128)(2,1)} %pad_maximum_fusion.1), channel_id=1, source_target_pairs={{8,0},{16,8},{24,16},{32,24},{40,32},{48,40},{56,48},{64,56},{72,6... | collective-permute-start | bytes 983048 | tf_op jit(solution)/shard_map/ppermute | solution.py:33
  21.8 11.5 %copy-start.3 = (bf16[512,160]{0,1:T(8,128)(2,1)S(1)}, bf16[512,160]{0,1:T(8,128)(2,1)}, u32[]{:S(2)}) copy-start(bf16[512,160]{0,1:T(8,128)(2,1)} %copy-done.2) | copy-start | bytes 491524
  21.8 11.5 %copy-start.5 = (bf16[512,160]{0,1:T(8,128)(2,1)S(1)}, bf16[512,160]{0,1:T(8,128)(2,1)}, u32[]{:S(2)}) copy-start(bf16[512,160]{0,1:T(8,128)(2,1)} %copy-done.4) | copy-start | bytes 491524
  50.8 25.1 %all-to-all-start = ((bf16[8,512,160]{1,2,0:T(8,128)(2,1)}), bf16[8,512,160]{1,2,0:T(8,128)(2,1)}, u32[]{:S(2)}, u32[]{:S(2)}) async-start(bf16[8,512,160]{1,2,0:T(8,128)(2,1)} %bitcast.106), calls=%async_computation | async-start | bytes 2621440 | tf_op jit(solution)/shard_map/all_to_all | solution.py:48
  79.2 8.6 %all-to-all-start.1 = ((f32[8,1,512]{2,1,0:T(1,128)}), f32[8,1,512]{2,1,0:T(1,128)S(1)}, u32[]{:S(2)}, u32[]{:S(2)}) async-start(f32[8,1,512]{2,1,0:T(1,128)} %broadcast_in_dim.98), calls=%async_computation.1 | async-start | bytes 32768 | tf_op jit(solution)/shard_map/all_to_all | solution.py:54
  180.3 4.6 %copy-start.6 = (s32[2048,1]{0,1:T(1,128)S(1)}, s32[2048,1]{0,1:T(1,128)}, u32[]{:S(2)}) copy-start(s32[2048,1]{0,1:T(1,128)} %param.28) | copy-start | bytes 24580
  180.3 31.8 %all-to-all-start.3 = ((bf16[8,128,1024]{2,1,0:T(8,128)(2,1)}), bf16[8,128,1024]{2,1,0:T(8,128)(2,1)}, u32[]{:S(2)}, u32[]{:S(2)}) async-start(bf16[8,128,1024]{2,1,0:T(8,128)(2,1)} %bitcast.105), calls=%async_computation.3 | async-start | bytes 4194304 | tf_op jit(solution)/shard_map/all_to_all | solution.py:48
  216.0 16.1 %all-to-all-start.4 = ((bf16[16,16,1024]{2,1,0:T(8,128)(2,1)}), bf16[16,16,1024]{2,1,0:T(8,128)(2,1)S(1)}, u32[]{:S(2)}, u32[]{:S(2)}) async-start(bf16[16,16,1024]{2,1,0:T(8,128)(2,1)} %bitcast.15), calls=%async_computation.4 | async-start | bytes 1048576 | tf_op jit(solution)/shard_map/all_to_all | solution.py:181
  237.6 5.0 %copy-start.9 = (s32[256]{0:T(256)S(1)}, s32[256]{0:T(256)}, u32[]{:S(2)}) copy-start(s32[256]{0:T(256)} %param.30) | copy-start | bytes 3076
  237.6 54.3 %all-to-all-start.5 = ((bf16[8,256,1024]{1,2,0:T(8,128)(2,1)}), bf16[8,256,1024]{1,2,0:T(8,128)(2,1)}, u32[]{:S(2)}, u32[]{:S(2)}) async-start(bf16[8,256,1024]{1,2,0:T(8,128)(2,1)} %stack.2), calls=%async_computation.5 | async-start | bytes 8388608 | tf_op jit(solution)/shard_map/all_to_all | solution.py:13
  242.3 53.0 %copy-start.7 = (f32[8192]{0:T(1024)S(1)}, f32[8192]{0:T(1024)}, u32[]{:S(2)}) copy-start(f32[8192]{0:T(1024)} %param.31) | copy-start | bytes 98308
  242.3 116.2 %reduce-scatter.2.cloned.1.call-start = ((), (), s32[]{:S(2)}) async-start(), calls=%async_computation.9 | async-start | bytes 4718592 | tf_op jit(solution)/shard_map/reduce_scatter | solution.py:236
  298.1 1.9 copy-start.1
Sparse Core Ops, SparseCore 0:
  9.5 67.2 all-gather.2
  78.9 87.3 all-gather.4
  324.3 34.1 reduce-scatter.1
